TPU v7x, 128 devices: a whole 4x4x4 slice. The times are simulated.
128 devices in a mesh: don: 8 (over x, core), acc: 16 (over y, z).
Axes of the slice: x: 4, y: 4, z: 4, core: 2. Of those that a mesh axis runs over, the one named last changes fastest.
Arguments:
- donor_emb: bfloat16 [262144, 768], P(('don', 'acc')), may hold values from -12 to 12
- acceptor_emb: bfloat16 [262144, 768], P(('don', 'acc')), may hold values from -6 to 6
- donor_pos: int32 [3072], P(('don', 'acc')), may hold values from 0 to 2047
- acceptor_pos: int32 [3072], P(('don', 'acc')), may hold values from 0 to 2047
- donor_count: int32 [128], P('don'), may hold values from 1 to 24, as said below
- acceptor_count: int32 [128], replicated, may hold values from 1 to 24, as said below
- target: int32 [64, 3072], P(None, 'don'), may hold values from 0 to 3071, as said below
- junction_mask: int32 [64, 3072], P(None, 'don'), may hold values 0 or 1
- weights: bfloat16 [64, 768, 768], P('acc'), may hold values from -1 to 2
Outputs:
- loss: float32 [], replicated
- grad_weight: float32 [768, 64, 768], P('don', 'acc')
Inputs may be any that keep to these rules, and one draw needn't show every extreme that they name: `donor_count`: the live donor slots of all shards number exactly 1600; some shard has all 24 live. `acceptor_count`: the live acceptor slots of all shards number exactly 1600; some shard has all 24 live. `target`: each entry names a live acceptor slot.
All inputs are finite; a program needn't handle non-finite values. No bound on the sum of `junction_mask` on one device may be relied on, other than what follows from the above.
Results may differ from a plain program's by a relative error of at most 0.0031.
Values may be sent and summed in bfloat16 or wider, within the bound.
No kernel may reach another device: no remote copies, remote signals or barrier semaphores. Data moves between devices by JAX's collectives and lax.ppermute only.
A program may use at most 128 MiB of HBM per device.

v0:
```python
import jax
import jax.numpy as jnp
from jax import lax
from jax.sharding import Mesh
from jax.sharding import PartitionSpec as P

ACC = ("acc_0", "acc_1")
DON = ("don_0", "don_1")
DON_ACC = ("don_0", "don_1", "acc_0", "acc_1")


def one_axis_at_a_time(shard, axes):
    for axis in axes:
        shard = lax.psum(shard, axis)
    return shard


def local(
    donor_emb,
    acceptor_emb,
    donor_pos,
    acceptor_pos,
    donor_count,
    acceptor_count,
    target,
    junction_mask,
    weights,
):
    slots = donor_pos.shape[0]
    width = weights.shape[1]
    tis_dev = weights.shape[0]
    scale = width ** (-0.5)
    column = lax.axis_index(ACC)
    donor_local = jnp.take(donor_emb, donor_pos, axis=0)
    acceptor_local = jnp.take(acceptor_emb, acceptor_pos, axis=0)
    donors = lax.all_gather(donor_local, ACC, axis=0, tiled=True)
    acceptors = lax.all_gather(acceptor_local, DON_ACC, axis=0, tiled=True)
    donor_rows = donors.shape[0]
    acceptor_rows = acceptors.shape[0]
    live_d = jnp.arange(donor_rows, dtype=jnp.int32) % slots < jnp.repeat(donor_count, slots)
    live_a = jnp.arange(acceptor_rows, dtype=jnp.int32) % slots < jnp.repeat(acceptor_count, slots)
    first_tissue = column * tis_dev
    targets_dev = lax.dynamic_slice_in_dim(target, first_tissue, tis_dev, 0)
    masks_dev = lax.dynamic_slice_in_dim(junction_mask, first_tissue, tis_dev, 0)
    weighting = jnp.where(live_d[None, :], masks_dev, 0).astype(jnp.float32)
    columns = jnp.arange(acceptor_rows, dtype=jnp.int32)

    def tissue(inputs):
        matrix, target_row, weight_row = inputs
        projected = jnp.dot(donors, matrix, preferred_element_type=jnp.float32).astype(jnp.bfloat16)
        scores = (
            lax.dot_general(
                projected, acceptors, (((1,), (1,)), ((), ())), preferred_element_type=jnp.float32
            )
            * scale
        )
        scores = jnp.where(live_a[None, :], scores, -1e30)
        highest = jnp.max(scores, axis=1, keepdims=True)
        summed_exp = jnp.sum(
            jnp.where(live_a[None, :], jnp.exp(scores - highest), 0.0), axis=1, keepdims=True
        )
        log_total = highest + jnp.log(summed_exp)
        is_target = columns[None, :] == target_row[:, None]
        picked = jnp.sum(jnp.where(is_target, scores, 0.0), axis=1)
        summed = jnp.sum(weight_row * (log_total[:, 0] - picked))
        counted = jnp.sum(weight_row)
        probs = jnp.where(live_a[None, :], jnp.exp(scores - log_total), 0.0)
        dscore = (weight_row[:, None] * (probs - is_target.astype(jnp.float32))).astype(
            jnp.bfloat16
        )
        dproj = (jnp.dot(dscore, acceptors, preferred_element_type=jnp.float32) * scale).astype(
            jnp.bfloat16
        )
        return (summed, counted, dproj)

    summed, counted, dproj = lax.map(tissue, (weights, targets_dev, weighting))
    summed, counted = (
        one_axis_at_a_time(jnp.sum(summed), DON_ACC),
        one_axis_at_a_time(jnp.sum(counted), DON_ACC),
    )
    loss = summed / jnp.maximum(counted, 1.0)
    grad_weight = lax.psum_scatter(
        jnp.einsum("nd,tne->dte", donors, dproj, preferred_element_type=jnp.float32),
        DON,
        scatter_dimension=0,
        tiled=True,
    )
    return (loss, grad_weight)


def solution(mesh):
    finer = Mesh(mesh.devices.reshape(4, 2, 4, 4), ("don_0", "don_1", "acc_0", "acc_1"))
    return jax.shard_map(
        local,
        mesh=finer,
        in_specs=(
            P(DON_ACC, None),
            P(DON_ACC, None),
            P(DON_ACC),
            P(DON_ACC),
            P(DON),
            P(),
            P(None, DON),
            P(None, DON),
            P(ACC, None, None),
        ),
        out_specs=(P(), P(DON, ACC, None)),
        check_vma=False,
    )
```

profile of v0, /device:TPU:1, one launch (start us, length us, event | category | flops | bytes accessed | tf_op | source)
XLA Modules:
  0.0 247.4 jit_solution(5175698280797513508)
XLA Ops:
  7.2 0.0 copy-start
  7.2 0.0 all-gather.2.cloned.1.call-start
  7.2 0.8 compare_select_fusion
  8.1 0.8 compare_and_fusion
  8.8 0.3 copy-done
  9.1 0.6 gather_fusion.1
  9.7 0.7 broadcast_select_fusion
  10.4 0.0 all-gather.2.cloned.1.call-update
  10.4 0.0 reduce-scatter.2.cloned.1.call-start
  10.5 0.7 broadcast_in_dim.75
  11.2 0.1 reshape.44
  11.3 2.9 %gather_fusion = bf16[24,768]{1,0:T(8,128)(2,1)S(1)} fusion(bf16[2048,768]{1,0:T(8,128)(2,1)} %param.13, s32[1024]{0:T(1024)S(1)} %pad_clamp_fusion.1), kind=kCustom, calls=%fused_computation.clone | custom fusion | bytes 73824 | tf_op jit(solution)/shard_map/jit(_take)/gather | solution.py:34
  14.3 0.1 broadcast_select_fusion.1
  14.3 23.8 %all_gather.6 = bf16[384,768]{1,0:T(8,128)(2,1)} all-gather(bf16[24,768]{1,0:T(8,128)(2,1)S(1)} %broadcast_select_fusion.1), channel_id=1, replica_groups=mesh['don_0'=4,'don_1'=2,'acc_0'=4,'acc_1'=4] {'acc_0','acc_1'}, dimensions={0}, use_global_device_ids=true | all-gather | bytes 626688 | tf_op jit(solution)/shard_map/all_gather | solution.py:36
  38.2 0.7 select_convert_fusion
  38.9 43.2 %all-gather.2.cloned.1.call-done = bf16[3072,768]{1,0:T(8,128)(2,1)} async-done(((bf16[24,768]{1,0:T(8,128)(2,1)}), bf16[3072,768]{1,0:T(8,128)(2,1)}) %all-gather.2.cloned.1.call-update) | async-done | bytes 4718608 | tf_op jit(solution)/shard_map/all_gather | solution.py:37
  82.1 91.8 %while.15 = (s32[]{:T(128)}, f32[4]{0:T(128)S(1)}, f32[4]{0:T(128)S(1)}, bf16[4,384,768]{2,1,0:T(8,128)(2,1)}, f32[4,384]{1,0:T(4,128)S(1)}, /*index=5*/bf16[4,7...) while((s32[]{:T(128)}, f32[4]{0:T(128)S(1)}, ...), condition=%wide.region_6.8_spmd.clone, body=%wide.region_0.7_spmd.clone.sunk | while | flops 4096644864 | bytes 26040484 | solution.py:76
  82.1 0.6 fusion.70
  82.7 0.7 broadcast_in_dim.138
  83.4 0.1 reshape.76
  83.5 7.9 %fusion.72 = (f32[384]{0:T(512)S(1)}, f32[384,3072]{1,0:T(8,128)}) fusion(bf16[3072,768]{1,0:T(8,128)(2,1)} %get-tuple-element.241, bf16[384,768]{1,0:T(8,128)(2,1)} %get-tuple-element.240, bf16[4,768,768]{2,1,0:T(8,128)(2,1)} %get-tuple-element.239, s32[]{:T(128)S(6)} %copy.20, pred[3072]{0:T(1024)(128)(4,1)S(1)} %fusion.71), kind=kOutput, calls=%fused_computation.58.clone.1 | convolution fusion | flops 2268757504 | bytes 11211268 | tf_op jit(solution)/shard_map/while/body/eval_jaxpr/dot_general | solution.py:52
  91.4 4.0 %fusion.73 = (f32[384]{0:T(512)S(1)}, f32[384]{0:T(512)S(1)}) fusion(f32[384,3072]{1,0:T(8,128)} %get-tuple-element.205, s32[384]{0:T(512)S(1)} %dynamic-slice_reduce_fusion.2, f32[384]{0:T(512)S(1)} %get-tuple-element.206, pred[3072]{0:T(1024)(128)(4,1)S(1)} %fusion.71), kind=kLoop, calls=%fused_computation.7.clone.1 | loop fusion | flops 7077120 | bytes 4727808 | tf_op jit(solution)/shard_map/while/body/eval_jaxpr/reduce_sum | solution.py:64
  95.4 0.7 multiply_reduce_fusion.2
  96.1 0.7 dynamic_update_slice.19
  96.8 0.8 dynamic_update_slice.20
  97.6 7.4 %fusion.74 = bf16[4,384,768]{2,1,0:T(8,128)(2,1)} fusion(bf16[4,384,768]{2,1,0:T(8,128)(2,1)} %get-tuple-element.226, s32[]{:T(128)S(6)} %copy.20, bf16[3072,768]{1,0:T(8,128)(2,1)} %get-tuple-element.241, f32[384,3072]{1,0:T(8,128)} %get-tuple-element.205, f32[384]{0:T(512)S(1)} %get-tuple-element.211, f32[384]{0:T(512)S(1)} %get-tuple-element.204, ...), kind=kOutput, calls=%fused_computation.23.clone.1 | convolution fusion | flops 1820786688 | bytes 10034692 | tf_op jit(solution)/shard_map/while/body/eval_jaxpr/dot_general | solution.py:71
  105.0 0.6 fusion.70
  105.6 0.7 broadcast_in_dim.138
  106.3 0.1 reshape.76
  106.5 7.9 %fusion.72 = (f32[384]{0:T(512)S(1)}, f32[384,3072]{1,0:T(8,128)}) fusion(bf16[3072,768]{1,0:T(8,128)(2,1)} %get-tuple-element.241, bf16[384,768]{1,0:T(8,128)(2,1)} %get-tuple-element.240, bf16[4,768,768]{2,1,0:T(8,128)(2,1)} %get-tuple-element.239, s32[]{:T(128)S(6)} %copy.20, pred[3072]{0:T(1024)(128)(4,1)S(1)} %fusion.71), kind=kOutput, calls=%fused_computation.58.clone.1 | convolution fusion | flops 2268757504 | bytes 11211268 | tf_op jit(solution)/shard_map/while/body/eval_jaxpr/dot_general | solution.py:52
  114.4 4.0 %fusion.73 = (f32[384]{0:T(512)S(1)}, f32[384]{0:T(512)S(1)}) fusion(f32[384,3072]{1,0:T(8,128)} %get-tuple-element.205, s32[384]{0:T(512)S(1)} %dynamic-slice_reduce_fusion.2, f32[384]{0:T(512)S(1)} %get-tuple-element.206, pred[3072]{0:T(1024)(128)(4,1)S(1)} %fusion.71), kind=kLoop, calls=%fused_computation.7.clone.1 | loop fusion | flops 7077120 | bytes 4727808 | tf_op jit(solution)/shard_map/while/body/eval_jaxpr/reduce_sum | solution.py:64
  118.4 0.7 multiply_reduce_fusion.2
  119.1 0.7 dynamic_update_slice.19
  119.8 0.8 dynamic_update_slice.20
  120.5 7.4 %fusion.74 = bf16[4,384,768]{2,1,0:T(8,128)(2,1)} fusion(bf16[4,384,768]{2,1,0:T(8,128)(2,1)} %get-tuple-element.226, s32[]{:T(128)S(6)} %copy.20, bf16[3072,768]{1,0:T(8,128)(2,1)} %get-tuple-element.241, f32[384,3072]{1,0:T(8,128)} %get-tuple-element.205, f32[384]{0:T(512)S(1)} %get-tuple-element.211, f32[384]{0:T(512)S(1)} %get-tuple-element.204, ...), kind=kOutput, calls=%fused_computation.23.clone.1 | convolution fusion | flops 1820786688 | bytes 10034692 | tf_op jit(solution)/shard_map/while/body/eval_jaxpr/dot_general | solution.py:71
  128.0 0.6 fusion.70
  128.6 0.7 broadcast_in_dim.138
  129.3 0.1 reshape.76
  129.4 7.9 %fusion.72 = (f32[384]{0:T(512)S(1)}, f32[384,3072]{1,0:T(8,128)}) fusion(bf16[3072,768]{1,0:T(8,128)(2,1)} %get-tuple-element.241, bf16[384,768]{1,0:T(8,128)(2,1)} %get-tuple-element.240, bf16[4,768,768]{2,1,0:T(8,128)(2,1)} %get-tuple-element.239, s32[]{:T(128)S(6)} %copy.20, pred[3072]{0:T(1024)(128)(4,1)S(1)} %fusion.71), kind=kOutput, calls=%fused_computation.58.clone.1 | convolution fusion | flops 2268757504 | bytes 11211268 | tf_op jit(solution)/shard_map/while/body/eval_jaxpr/dot_general | solution.py:52
  137.3 4.0 %fusion.73 = (f32[384]{0:T(512)S(1)}, f32[384]{0:T(512)S(1)}) fusion(f32[384,3072]{1,0:T(8,128)} %get-tuple-element.205, s32[384]{0:T(512)S(1)} %dynamic-slice_reduce_fusion.2, f32[384]{0:T(512)S(1)} %get-tuple-element.206, pred[3072]{0:T(1024)(128)(4,1)S(1)} %fusion.71), kind=kLoop, calls=%fused_computation.7.clone.1 | loop fusion | flops 7077120 | bytes 4727808 | tf_op jit(solution)/shard_map/while/body/eval_jaxpr/reduce_sum | solution.py:64
  141.3 0.7 multiply_reduce_fusion.2
  142.0 0.7 dynamic_update_slice.19
  142.7 0.8 dynamic_update_slice.20
  143.5 7.5 %fusion.74 = bf16[4,384,768]{2,1,0:T(8,128)(2,1)} fusion(bf16[4,384,768]{2,1,0:T(8,128)(2,1)} %get-tuple-element.226, s32[]{:T(128)S(6)} %copy.20, bf16[3072,768]{1,0:T(8,128)(2,1)} %get-tuple-element.241, f32[384,3072]{1,0:T(8,128)} %get-tuple-element.205, f32[384]{0:T(512)S(1)} %get-tuple-element.211, f32[384]{0:T(512)S(1)} %get-tuple-element.204, ...), kind=kOutput, calls=%fused_computation.23.clone.1 | convolution fusion | flops 1820786688 | bytes 10034692 | tf_op jit(solution)/shard_map/while/body/eval_jaxpr/dot_general | solution.py:71
  150.9 0.6 fusion.70
  151.5 0.7 broadcast_in_dim.138
  152.3 0.1 reshape.76
  152.4 7.9 %fusion.72 = (f32[384]{0:T(512)S(1)}, f32[384,3072]{1,0:T(8,128)}) fusion(bf16[3072,768]{1,0:T(8,128)(2,1)} %get-tuple-element.241, bf16[384,768]{1,0:T(8,128)(2,1)} %get-tuple-element.240, bf16[4,768,768]{2,1,0:T(8,128)(2,1)} %get-tuple-element.239, s32[]{:T(128)S(6)} %copy.20, pred[3072]{0:T(1024)(128)(4,1)S(1)} %fusion.71), kind=kOutput, calls=%fused_computation.58.clone.1 | convolution fusion | flops 2268757504 | bytes 11211268 | tf_op jit(solution)/shard_map/while/body/eval_jaxpr/dot_general | solution.py:52
  160.3 4.0 %fusion.73 = (f32[384]{0:T(512)S(1)}, f32[384]{0:T(512)S(1)}) fusion(f32[384,3072]{1,0:T(8,128)} %get-tuple-element.205, s32[384]{0:T(512)S(1)} %dynamic-slice_reduce_fusion.2, f32[384]{0:T(512)S(1)} %get-tuple-element.206, pred[3072]{0:T(1024)(128)(4,1)S(1)} %fusion.71), kind=kLoop, calls=%fused_computation.7.clone.1 | loop fusion | flops 7077120 | bytes 4727808 | tf_op jit(solution)/shard_map/while/body/eval_jaxpr/reduce_sum | solution.py:64
  164.3 0.7 multiply_reduce_fusion.2
  165.0 0.7 dynamic_update_slice.19
  165.7 0.8 dynamic_update_slice.20
  166.5 7.4 %fusion.74 = bf16[4,384,768]{2,1,0:T(8,128)(2,1)} fusion(bf16[4,384,768]{2,1,0:T(8,128)(2,1)} %get-tuple-element.226, s32[]{:T(128)S(6)} %copy.20, bf16[3072,768]{1,0:T(8,128)(2,1)} %get-tuple-element.241, f32[384,3072]{1,0:T(8,128)} %get-tuple-element.205, f32[384]{0:T(512)S(1)} %get-tuple-element.211, f32[384]{0:T(512)S(1)} %get-tuple-element.204, ...), kind=kOutput, calls=%fused_computation.23.clone.1 | convolution fusion | flops 1820786688 | bytes 10034692 | tf_op jit(solution)/shard_map/while/body/eval_jaxpr/dot_general | solution.py:71
  173.9 8.1 %fusion.42 = f32[768,4,768]{2,0,1:T(8,128)} fusion(bf16[4,384,768]{2,1,0:T(8,128)(2,1)} %get-tuple-element.64, bf16[384,768]{1,0:T(8,128)(2,1)} %get-tuple-element.249), kind=kOutput, calls=%fused_computation.40 | convolution fusion | flops 1811939328 | bytes 12386304 | tf_op jit(solution)/shard_map/nd,tne->dte/dot_general | solution.py:83
  182.0 0.0 reduce-scatter.2.cloned.1.call-update
  182.1 0.6 reduce_sum.54
  182.7 0.6 reduce_sum.55
  183.3 7.4 %all-reduce.2 = (f32[]{:T(128)}, f32[]{:T(128)}) all-reduce(f32[]{:T(128)} %reduce_sum.54, f32[]{:T(128)} %reduce_sum.55), channel_id=1, replica_groups=mesh['don_0'=4,'don_1'=2,'acc_0'=4,'acc_1'=4] {'don_0'}, use_global_device_ids=true, to_apply=%region_8.10 | all-reduce | flops 2 | bytes 16 | tf_op jit(solution)/shard_map/psum | solution.py:14
  190.7 5.0 %all-reduce.3 = (f32[]{:T(128)}, f32[]{:T(128)}) all-reduce(f32[]{:T(128)} %get-tuple-element.121, f32[]{:T(128)} %get-tuple-element.122), channel_id=1, replica_groups=mesh['don_0'=4,'don_1'=2,'acc_0'=4,'acc_1'=4] {'don_1'}, use_global_device_ids=true, to_apply=%region_9.11 | all-reduce | flops 2 | bytes 16 | tf_op jit(solution)/shard_map/psum | solution.py:14
  195.7 9.4 %all-reduce.1 = (f32[]{:T(128)}, f32[]{:T(128)}) all-reduce(f32[]{:T(128)} %get-tuple-element.123, f32[]{:T(128)} %get-tuple-element.124), channel_id=1, replica_groups=mesh['don_0'=4,'don_1'=2,'acc_0'=4,'acc_1'=4] {'acc_0'}, use_global_device_ids=true, to_apply=%region_10.12 | all-reduce | flops 2 | bytes 16 | tf_op jit(solution)/shard_map/psum | solution.py:14
  205.1 8.1 %all-reduce = (f32[]{:T(128)}, f32[]{:T(128)}) all-reduce(f32[]{:T(128)} %get-tuple-element.119, f32[]{:T(128)} %get-tuple-element.120), channel_id=1, replica_groups=mesh['don_0'=4,'don_1'=2,'acc_0'=4,'acc_1'=4] {'acc_1'}, use_global_device_ids=true, to_apply=%region_11.13 | all-reduce | flops 2 | bytes 16 | tf_op jit(solution)/shard_map/psum | solution.py:14
  214.5 21.8 %reduce-scatter.2.cloned.1.call-done = f32[96,4,768]{2,0,1:T(8,128)} async-done(((f32[768,4,768]{2,0,1:T(8,128)}), f32[96,4,768]{2,0,1:T(8,128)}) %reduce-scatter.2.cloned.1.call-update) | async-done | bytes 1179664 | tf_op jit(solution)/shard_map/reduce_scatter | solution.py:82
  236.4 3.0 %copy.12 = f32[96,4,768]{2,1,0:T(4,128)} copy(f32[96,4,768]{2,0,1:T(8,128)} %reduce-scatter.2.cloned.1.call-done) | data formatting | bytes 2359296
  (14 shorter events, 0.2 us)
Async XLA Ops:
  7.2 1.9 copy-start
  7.2 74.9 %all-gather.2.cloned.1.call-start = ((), (), s32[]{:S(2)}) async-start(), calls=%async_computation.1 | async-start | bytes 4755456 | tf_op jit(solution)/shard_map/all_gather | solution.py:37
  10.4 226.0 %reduce-scatter.2.cloned.1.call-start = ((), (), s32[]{:S(2)}) async-start(), calls=%async_computation.2 | async-start | bytes 10616832 | tf_op jit(solution)/shard_map/reduce_scatter | solution.py:82
Sparse Core Ops, SparseCore 0:
  11.7 70.3 all-gather.1
  182.2 54.1 reduce-scatter.1
where the time goes:
time: 248 us; the launch traced here: 247 us
  matrix products  69.4 us (28%)
  waiting for transfers between devices  65 us (26%)
  blocking collectives  53.8 us (22%)
  other arithmetic  25.5 us (10%)
  local copies, waits for them, and re-layouts  17 us (7%)
  between operations  16.5 us (7%)
    all_gather x1, waiting for transfers between devices, local(): acceptors = lax.all_gather(acceptor_local, DON_ACC, axis=0, tiled=True)  43.2 us
    dot_general x4, matrix products, tissue(): lax.dot_general(projected, acceptors, (((1,), (1,)), ((), ())), preferred...  31.5 us
    psum x4, blocking collectives, one_axis_at_a_time(): shard = lax.psum(shard, axis)  30 us
    dot_general x4, matrix products, tissue(): jnp.dot(dscore, acceptors, preferred_element_type=jnp.float32) * scale  29.8 us
    all_gather x1, blocking collectives, local(): donors = lax.all_gather(donor_local, ACC, axis=0, tiled=True)  23.8 us
    reduce_scatter x1, waiting for transfers between devices, local(): lax.psum_scatter(jnp.einsum('nd,tne->dte', donors, dproj, preferred_eleme...  21.8 us
    reduce_sum x4, other arithmetic, tissue(): picked = jnp.sum(jnp.where(is_target, scores, 0.0), axis=1)  16 us
    dot_general x1, matrix products, local(): jnp.einsum('nd,tne->dte', donors, dproj, preferred_element_type=jnp.float32)  8.13 us
  transfers between devices with their start and end apart: 2, of which 2 were waited for; matrix products, arithmetic and copies ran while one was open for 2% of the time, Pallas kernels for 0%

commit v1 on v0

--- a/solution.py
+++ b/solution.py
@@ -11,7 +11,8 @@
 
 def one_axis_at_a_time(shard, axes):
     for axis in axes:
-        shard = lax.psum(shard, axis)
+        parts = lax.all_gather(shard, axis)
+        shard = jnp.sum(parts, axis=0)
     return shard
 
 

time: 248 us -> 243 us (0.980)
  waiting for transfers between devices: 65 us -> 48 us
  local copies, waits for them, and re-layouts: 17 us -> 31.4 us
  other arithmetic: 25.5 us -> 31.2 us
  matrix products: 69.4 us -> 63.9 us
    psum x4 -> x0, blocking collectives: 30 us -> none  [one_axis_at_a_time(): shard = lax.psum(shard, axis)]
    unnamed x0 -> x4, blocking collectives: none -> 27.5 us
    reduce_scatter x1, waiting for transfers between devices: 21.8 us -> 4.83 us  [local(): lax.psum_scatter(jnp.einsum('nd,tne->dte', donors, dproj, preferred_eleme...]
    unnamed x3 -> x33, local copies, waits for them, and re-layouts: 3.31 us -> 17.7 us
    dot_general x4, matrix products: 29.8 us -> 24.2 us  [tissue(): jnp.dot(dscore, acceptors, preferred_element_type=jnp.float32) * scale]
    reduce_sum x0 -> x8, other arithmetic: none -> 5.05 us  [one_axis_at_a_time(): shard = jnp.sum(parts, axis=0)]
  transfers between devices with their start and end apart: 2 -> 2, of which waited for: 2 -> 2; matrix products, arithmetic and copies ran while one was open for 2% -> 10% of each run, Pallas kernels for 0% -> 0%
where the time goes in v1:
time: 243 us
  matrix products  63.9 us (26%)
  blocking collectives  51.4 us (21%)
  waiting for transfers between devices  48 us (20%)
  local copies, waits for them, and re-layouts  31.4 us (13%)
  other arithmetic  31.2 us (13%)
  between operations  16.6 us (7%)
    all_gather x1, waiting for transfers between devices, local(): acceptors = lax.all_gather(acceptor_local, DON_ACC, axis=0, tiled=True)  43.2 us
    dot_general x4, matrix products, tissue(): lax.dot_general(projected, acceptors, (((1,), (1,)), ((), ())), preferred...  31.5 us
    unnamed x4, blocking collectives  27.5 us
    dot_general x4, matrix products, tissue(): jnp.dot(dscore, acceptors, preferred_element_type=jnp.float32) * scale  24.2 us
    all_gather x1, blocking collectives, local(): donors = lax.all_gather(donor_local, ACC, axis=0, tiled=True)  23.8 us
    unnamed x33, local copies, waits for them, and re-layouts  17.7 us
    reduce_sum x4, other arithmetic, tissue(): picked = jnp.sum(jnp.where(is_target, scores, 0.0), axis=1)  16.5 us
    dot_general x1, matrix products, local(): jnp.einsum('nd,tne->dte', donors, dproj, preferred_element_type=jnp.float32)  8.13 us
  transfers between devices with their start and end apart: 2, of which 2 were waited for; matrix products, arithmetic and copies ran while one was open for 10% of the time, Pallas kernels for 0%

profile of v1, /device:TPU:1, one launch (start us, length us, event | category | flops | bytes accessed | tf_op | source)
XLA Modules:
  0.0 242.5 jit_solution(16570760462636401974)
XLA Ops:
  7.2 0.8 compare_select_fusion
  8.1 0.8 compare_and_fusion
  9.1 0.6 gather_fusion.1
  9.7 0.7 broadcast_select_fusion
  10.5 0.7 broadcast_in_dim.75
  11.3 2.9 %gather_fusion = bf16[24,768]{1,0:T(8,128)(2,1)S(1)} fusion(bf16[2048,768]{1,0:T(8,128)(2,1)} %param.13, s32[1024]{0:T(1024)S(1)} %pad_clamp_fusion.1), kind=kCustom, calls=%fused_computation.clone | custom fusion | bytes 73824 | tf_op jit(solution)/shard_map/jit(_take)/gather | solution.py:35
  14.3 23.8 %all_gather.54 = bf16[384,768]{1,0:T(8,128)(2,1)} all-gather(bf16[24,768]{1,0:T(8,128)(2,1)S(1)} %broadcast_select_fusion.1), channel_id=1, replica_groups=mesh['don_0'=4,'don_1'=2,'acc_0'=4,'acc_1'=4] {'acc_0','acc_1'}, dimensions={0}, use_global_device_ids=true | all-gather | bytes 626688 | tf_op jit(solution)/shard_map/all_gather | solution.py:37
  38.2 0.7 select_convert_fusion
  38.9 43.2 %all-gather.2.cloned.1.call-done = bf16[3072,768]{1,0:T(8,128)(2,1)} async-done(((bf16[24,768]{1,0:T(8,128)(2,1)}), bf16[3072,768]{1,0:T(8,128)(2,1)}) %all-gather.2.cloned.1.call-update) | async-done | bytes 4718608 | tf_op jit(solution)/shard_map/all_gather | solution.py:38
  82.1 86.9 %while.15 = (s32[]{:T(128)}, f32[4]{0:T(128)S(1)}, f32[4]{0:T(128)S(1)}, bf16[4,384,768]{2,1,0:T(8,128)(2,1)}, f32[4,384]{1,0:T(4,128)S(1)}, /*index=5*/bf16[4,7...) while((s32[]{:T(128)}, f32[4]{0:T(128)S(1)}, ...), condition=%wide.region_6.8_spmd.clone, body=%wide.region_0.7_spmd.clone.sunk | while | flops 4096644864 | bytes 44915888 | solution.py:77
  82.1 0.7 broadcast_in_dim.138
  82.9 7.9 %fusion.72 = (f32[384]{0:T(512)S(1)}, f32[384,3072]{1,0:T(8,128)}) fusion(bf16[3072,768]{1,0:T(8,128)(2,1)} %get-tuple-element.241, bf16[384,768]{1,0:T(8,128)(2,1)} %get-tuple-element.240, bf16[4,768,768]{2,1,0:T(8,128)(2,1)} %get-tuple-element.239, s32[]{:T(128)} %get-tuple-element.223, pred[3072]{0:T(1024)(128)(4,1)S(1)} %fusion.71), kind=kOutput, calls=%fused_computation.58.clone.1 | convolution fusion | flops 2268757504 | bytes 11211776 | tf_op jit(solution)/shard_map/while/body/eval_jaxpr/dot_general | solution.py:53
  90.8 4.1 %fusion.73 = (f32[384]{0:T(512)S(1)}, f32[384]{0:T(512)S(1)}) fusion(f32[384,3072]{1,0:T(8,128)} %get-tuple-element.205, s32[384]{0:T(512)S(1)} %dynamic-slice_reduce_fusion.2, f32[384]{0:T(512)S(1)} %get-tuple-element.206, pred[3072]{0:T(1024)(128)(4,1)S(1)} %fusion.71), kind=kLoop, calls=%fused_computation.7.clone.1 | loop fusion | flops 7077120 | bytes 4727808 | tf_op jit(solution)/shard_map/while/body/eval_jaxpr/reduce_sum | solution.py:65
  95.0 0.6 fusion.70
  95.6 0.7 multiply_reduce_fusion.2
  96.3 6.0 %fusion.74 = bf16[4,384,768]{2,1,0:T(8,128)(2,1)} fusion(bf16[4,384,768]{2,1,0:T(8,128)(2,1)} %get-tuple-element.226, s32[]{:T(128)} %get-tuple-element.223, bf16[3072,768]{1,0:T(8,128)(2,1)} %get-tuple-element.241, f32[384,3072]{1,0:T(8,128)S(1)} %copy-done.1, f32[384]{0:T(512)S(1)} %get-tuple-element.211, f32[384]{0:T(512)S(1)} %get-tuple-element.204, ...), kind=kOutput, calls=%fused_computation.23.clone.1 | convolution fusion | flops 1820786688 | bytes 10035200 | tf_op jit(solution)/shard_map/while/body/eval_jaxpr/dot_general | solution.py:72
  102.3 0.7 dynamic_update_slice.19
  103.0 0.8 dynamic_update_slice.20
  103.8 0.7 broadcast_in_dim.138
  104.6 7.9 %fusion.72 = (f32[384]{0:T(512)S(1)}, f32[384,3072]{1,0:T(8,128)}) fusion(bf16[3072,768]{1,0:T(8,128)(2,1)} %get-tuple-element.241, bf16[384,768]{1,0:T(8,128)(2,1)} %get-tuple-element.240, bf16[4,768,768]{2,1,0:T(8,128)(2,1)} %get-tuple-element.239, s32[]{:T(128)} %get-tuple-element.223, pred[3072]{0:T(1024)(128)(4,1)S(1)} %fusion.71), kind=kOutput, calls=%fused_computation.58.clone.1 | convolution fusion | flops 2268757504 | bytes 11211776 | tf_op jit(solution)/shard_map/while/body/eval_jaxpr/dot_general | solution.py:53
  112.6 4.1 %fusion.73 = (f32[384]{0:T(512)S(1)}, f32[384]{0:T(512)S(1)}) fusion(f32[384,3072]{1,0:T(8,128)} %get-tuple-element.205, s32[384]{0:T(512)S(1)} %dynamic-slice_reduce_fusion.2, f32[384]{0:T(512)S(1)} %get-tuple-element.206, pred[3072]{0:T(1024)(128)(4,1)S(1)} %fusion.71), kind=kLoop, calls=%fused_computation.7.clone.1 | loop fusion | flops 7077120 | bytes 4727808 | tf_op jit(solution)/shard_map/while/body/eval_jaxpr/reduce_sum | solution.py:65
  116.7 0.6 fusion.70
  117.3 0.7 multiply_reduce_fusion.2
  118.0 6.0 %fusion.74 = bf16[4,384,768]{2,1,0:T(8,128)(2,1)} fusion(bf16[4,384,768]{2,1,0:T(8,128)(2,1)} %get-tuple-element.226, s32[]{:T(128)} %get-tuple-element.223, bf16[3072,768]{1,0:T(8,128)(2,1)} %get-tuple-element.241, f32[384,3072]{1,0:T(8,128)S(1)} %copy-done.1, f32[384]{0:T(512)S(1)} %get-tuple-element.211, f32[384]{0:T(512)S(1)} %get-tuple-element.204, ...), kind=kOutput, calls=%fused_computation.23.clone.1 | convolution fusion | flops 1820786688 | bytes 10035200 | tf_op jit(solution)/shard_map/while/body/eval_jaxpr/dot_general | solution.py:72
  124.0 0.7 dynamic_update_slice.19
  124.8 0.8 dynamic_update_slice.20
  125.5 0.7 broadcast_in_dim.138
  126.4 7.9 %fusion.72 = (f32[384]{0:T(512)S(1)}, f32[384,3072]{1,0:T(8,128)}) fusion(bf16[3072,768]{1,0:T(8,128)(2,1)} %get-tuple-element.241, bf16[384,768]{1,0:T(8,128)(2,1)} %get-tuple-element.240, bf16[4,768,768]{2,1,0:T(8,128)(2,1)} %get-tuple-element.239, s32[]{:T(128)} %get-tuple-element.223, pred[3072]{0:T(1024)(128)(4,1)S(1)} %fusion.71), kind=kOutput, calls=%fused_computation.58.clone.1 | convolution fusion | flops 2268757504 | bytes 11211776 | tf_op jit(solution)/shard_map/while/body/eval_jaxpr/dot_general | solution.py:53
  134.3 4.1 %fusion.73 = (f32[384]{0:T(512)S(1)}, f32[384]{0:T(512)S(1)}) fusion(f32[384,3072]{1,0:T(8,128)} %get-tuple-element.205, s32[384]{0:T(512)S(1)} %dynamic-slice_reduce_fusion.2, f32[384]{0:T(512)S(1)} %get-tuple-element.206, pred[3072]{0:T(1024)(128)(4,1)S(1)} %fusion.71), kind=kLoop, calls=%fused_computation.7.clone.1 | loop fusion | flops 7077120 | bytes 4727808 | tf_op jit(solution)/shard_map/while/body/eval_jaxpr/reduce_sum | solution.py:65
  138.4 0.6 fusion.70
  139.0 0.7 multiply_reduce_fusion.2
  139.7 6.1 %fusion.74 = bf16[4,384,768]{2,1,0:T(8,128)(2,1)} fusion(bf16[4,384,768]{2,1,0:T(8,128)(2,1)} %get-tuple-element.226, s32[]{:T(128)} %get-tuple-element.223, bf16[3072,768]{1,0:T(8,128)(2,1)} %get-tuple-element.241, f32[384,3072]{1,0:T(8,128)S(1)} %copy-done.1, f32[384]{0:T(512)S(1)} %get-tuple-element.211, f32[384]{0:T(512)S(1)} %get-tuple-element.204, ...), kind=kOutput, calls=%fused_computation.23.clone.1 | convolution fusion | flops 1820786688 | bytes 10035200 | tf_op jit(solution)/shard_map/while/body/eval_jaxpr/dot_general | solution.py:72
  145.8 0.7 dynamic_update_slice.19
  146.5 0.8 dynamic_update_slice.20
  147.3 0.7 broadcast_in_dim.138
  148.1 7.9 %fusion.72 = (f32[384]{0:T(512)S(1)}, f32[384,3072]{1,0:T(8,128)}) fusion(bf16[3072,768]{1,0:T(8,128)(2,1)} %get-tuple-element.241, bf16[384,768]{1,0:T(8,128)(2,1)} %get-tuple-element.240, bf16[4,768,768]{2,1,0:T(8,128)(2,1)} %get-tuple-element.239, s32[]{:T(128)} %get-tuple-element.223, pred[3072]{0:T(1024)(128)(4,1)S(1)} %fusion.71), kind=kOutput, calls=%fused_computation.58.clone.1 | convolution fusion | flops 2268757504 | bytes 11211776 | tf_op jit(solution)/shard_map/while/body/eval_jaxpr/dot_general | solution.py:53
  156.0 4.1 %fusion.73 = (f32[384]{0:T(512)S(1)}, f32[384]{0:T(512)S(1)}) fusion(f32[384,3072]{1,0:T(8,128)} %get-tuple-element.205, s32[384]{0:T(512)S(1)} %dynamic-slice_reduce_fusion.2, f32[384]{0:T(512)S(1)} %get-tuple-element.206, pred[3072]{0:T(1024)(128)(4,1)S(1)} %fusion.71), kind=kLoop, calls=%fused_computation.7.clone.1 | loop fusion | flops 7077120 | bytes 4727808 | tf_op jit(solution)/shard_map/while/body/eval_jaxpr/reduce_sum | solution.py:65
  160.2 0.6 fusion.70
  160.8 0.7 multiply_reduce_fusion.2
  161.4 6.1 %fusion.74 = bf16[4,384,768]{2,1,0:T(8,128)(2,1)} fusion(bf16[4,384,768]{2,1,0:T(8,128)(2,1)} %get-tuple-element.226, s32[]{:T(128)} %get-tuple-element.223, bf16[3072,768]{1,0:T(8,128)(2,1)} %get-tuple-element.241, f32[384,3072]{1,0:T(8,128)S(1)} %copy-done.1, f32[384]{0:T(512)S(1)} %get-tuple-element.211, f32[384]{0:T(512)S(1)} %get-tuple-element.204, ...), kind=kOutput, calls=%fused_computation.23.clone.1 | convolution fusion | flops 1820786688 | bytes 10035200 | tf_op jit(solution)/shard_map/while/body/eval_jaxpr/dot_general | solution.py:72
  167.5 0.7 dynamic_update_slice.19
  168.2 0.8 dynamic_update_slice.20
  169.0 8.1 %fusion.42 = f32[768,4,768]{2,0,1:T(8,128)} fusion(bf16[4,384,768]{2,1,0:T(8,128)(2,1)} %get-tuple-element.64, bf16[384,768]{1,0:T(8,128)(2,1)} %get-tuple-element.249), kind=kOutput, calls=%fused_computation.40 | convolution fusion | flops 1811939328 | bytes 12386304 | tf_op jit(solution)/shard_map/nd,tne->dte/dot_general | solution.py:84
  177.2 0.6 copy-done.5
  178.4 0.7 reduce_sum.131
  179.6 1.4 dynamic-update-slice.4
  181.1 1.4 dynamic-update-slice
  183.1 7.4 %all-reduce.10 = (f32[4]{0:T(128)S(1)}, f32[4]{0:T(128)S(1)}) all-reduce(f32[4]{0:T(128)S(1)} %dynamic-update-slice, f32[4]{0:T(128)S(1)} %dynamic-update-slice.4), channel_id=1, replica_groups=mesh['don_0'=4,'don_1'=2,'acc_0'=4,'acc_1'=4] {'don_0'}, use_global_device_ids=true, to_apply=%add | all-reduce | flops 8 | bytes 64
  190.5 0.7 reduce_sum.132
  191.7 1.4 dynamic-update-slice.5
  193.2 1.4 dynamic-update-slice.1
  195.2 4.0 %all-reduce.11 = (f32[2]{0:T(128)S(1)}, f32[2]{0:T(128)S(1)}) all-reduce(f32[2]{0:T(128)S(1)} %dynamic-update-slice.1, f32[2]{0:T(128)S(1)} %dynamic-update-slice.5), channel_id=1, replica_groups=mesh['don_0'=4,'don_1'=2,'acc_0'=4,'acc_1'=4] {'don_1'}, use_global_device_ids=true, to_apply=%add.1 | all-reduce | flops 4 | bytes 32
  199.2 0.7 reduce_sum.133
  200.5 1.4 dynamic-update-slice.6
  201.9 1.4 dynamic-update-slice.2
  203.9 8.7 %all-reduce.9 = (f32[4]{0:T(128)S(1)}, f32[4]{0:T(128)S(1)}) all-reduce(f32[4]{0:T(128)S(1)} %dynamic-update-slice.2, f32[4]{0:T(128)S(1)} %dynamic-update-slice.6), channel_id=1, replica_groups=mesh['don_0'=4,'don_1'=2,'acc_0'=4,'acc_1'=4] {'acc_0'}, use_global_device_ids=true, to_apply=%add.2 | all-reduce | flops 8 | bytes 64
  212.6 0.7 reduce_sum.134
  213.9 1.4 dynamic-update-slice.7
  215.4 1.4 dynamic-update-slice.3
  216.8 7.4 %all-reduce.8 = (f32[4]{0:T(128)S(1)}, f32[4]{0:T(128)S(1)}) all-reduce(f32[4]{0:T(128)S(1)} %dynamic-update-slice.3, f32[4]{0:T(128)S(1)} %dynamic-update-slice.7), channel_id=1, replica_groups=mesh['don_0'=4,'don_1'=2,'acc_0'=4,'acc_1'=4] {'acc_1'}, use_global_device_ids=true, to_apply=%add.3 | all-reduce | flops 8 | bytes 64
  224.2 0.6 reduce_sum.135
  225.4 0.6 reduce_sum.130
  226.7 4.8 %reduce-scatter.2.cloned.1.call-done = f32[96,4,768]{2,0,1:T(8,128)} async-done(((f32[768,4,768]{2,0,1:T(8,128)}), f32[96,4,768]{2,0,1:T(8,128)}) %reduce-scatter.2.cloned.1.call-update) | async-done | bytes 1179664 | tf_op jit(solution)/shard_map/reduce_scatter | solution.py:83
  231.5 3.0 %copy.12 = f32[96,4,768]{2,1,0:T(4,128)} copy(f32[96,4,768]{2,0,1:T(8,128)} %reduce-scatter.2.cloned.1.call-done) | data formatting | bytes 2359296
  (57 shorter events, 5.9 us)
Async XLA Ops:
  7.2 1.9 copy-start
  7.2 74.9 %all-gather.2.cloned.1.call-start = ((), (), s32[]{:S(2)}) async-start(), calls=%async_computation.1 | async-start | bytes 4755456 | tf_op jit(solution)/shard_map/all_gather | solution.py:38
  10.4 221.1 %reduce-scatter.2.cloned.1.call-start = ((), (), s32[]{:S(2)}) async-start(), calls=%async_computation.2 | async-start | bytes 10616832 | tf_op jit(solution)/shard_map/reduce_scatter | solution.py:83
  90.8 5.5 %copy-start.1 = (f32[384,3072]{1,0:T(8,128)S(1)}, f32[384,3072]{1,0:T(8,128)}, u32[]{:S(2)}) copy-start(f32[384,3072]{1,0:T(8,128)} %get-tuple-element.205) | copy-start | bytes 14155780 | tf_op jit(solution)/shard_map/while
  112.5 5.5 %copy-start.1 = (f32[384,3072]{1,0:T(8,128)S(1)}, f32[384,3072]{1,0:T(8,128)}, u32[]{:S(2)}) copy-start(f32[384,3072]{1,0:T(8,128)} %get-tuple-element.205) | copy-start | bytes 14155780 | tf_op jit(solution)/shard_map/while
  134.2 5.5 %copy-start.1 = (f32[384,3072]{1,0:T(8,128)S(1)}, f32[384,3072]{1,0:T(8,128)}, u32[]{:S(2)}) copy-start(f32[384,3072]{1,0:T(8,128)} %get-tuple-element.205) | copy-start | bytes 14155780 | tf_op jit(solution)/shard_map/while
  156.0 5.5 %copy-start.1 = (f32[384,3072]{1,0:T(8,128)S(1)}, f32[384,3072]{1,0:T(8,128)}, u32[]{:S(2)}) copy-start(f32[384,3072]{1,0:T(8,128)} %get-tuple-element.205) | copy-start | bytes 14155780 | tf_op jit(solution)/shard_map/while
  177.1 0.7 copy-start.5
  177.1 5.4 %copy-start.4 = (u32[128]{0:T(128)S(1)}, u32[128]{0:T(128)}, u32[]{:S(2)}) copy-start(u32[128]{0:T(128)} %constant.79) | copy-start | bytes 1540
  177.1 17.5 %copy-start.3 = (u32[128]{0:T(128)S(1)}, u32[128]{0:T(128)}, u32[]{:S(2)}) copy-start(u32[128]{0:T(128)} %constant.84) | copy-start | bytes 1540
  177.1 26.2 %copy-start.2 = (u32[128]{0:T(128)S(1)}, u32[128]{0:T(128)}, u32[]{:S(2)}) copy-start(u32[128]{0:T(128)} %constant.89) | copy-start | bytes 1540
Sparse Core Ops, SparseCore 0:
  11.7 70.3 all-gather.1
  177.3 54.2 reduce-scatter.1
